TPU v7x, 32 devices: a whole 2x2x4 slice. The times are simulated.
32 devices in a mesh: tp: 8 (over z, y), dp: 4 (over x, core).
Axes of the slice: x: 2, y: 2, z: 4, core: 2. Of those that a mesh axis runs over, the one named last changes fastest.
Arguments:
- tokens: bfloat16 [768, 4096], P(('dp', 'tp')), may hold values from -6 to 6
- hidden_grad: bfloat16 [768, 14336], P('dp', 'tp'), may hold values from -0.59765625 to 0.59765625
- gate_value: bfloat16 [768, 14336], P('dp', 'tp'), may hold values from -6 to 6
- up_value: bfloat16 [768, 14336], P('dp', 'tp'), may hold values from -6 to 6
- gate_weight: bfloat16 [4096, 14336], P('dp', 'tp'), may hold values from -0.09375 to 0.09375
- up_weight: bfloat16 [4096, 14336], P('dp', 'tp'), may hold values from -0.09375 to 0.09375
Outputs:
- input_grad: bfloat16 [768, 4096], P(('dp', 'tp'))
- gate_grad: bfloat16 [4096, 14336], P('dp', 'tp')
- up_grad: bfloat16 [4096, 14336], P('dp', 'tp')
All inputs are finite; a program needn't handle non-finite values.
Results may differ from a plain program's by a relative error of at most 0.018.
Values may be sent and summed in bfloat16 or wider, within the bound.
A program may use at most 128 MiB of HBM per device.

v0:
```python
import jax
import jax.numpy as jnp
from jax import lax
from jax.sharding import PartitionSpec as P


def on_device(tokens, hidden_grad, gate_value, up_value, gate_weight, up_weight):
    n_dp = lax.axis_size("dp")
    n_tp = lax.axis_size("tp")
    token_rows, features = tokens.shape
    width = gate_weight.shape[0]
    hidden_width = gate_value.shape[1]
    gate_float = gate_value.astype(jnp.float32)
    up_float = up_value.astype(jnp.float32)
    logistic = jax.nn.sigmoid(gate_float)
    upstream = hidden_grad.astype(jnp.float32)
    d_gate = (upstream * up_float * logistic * (1.0 + gate_float * (1.0 - logistic))).astype(
        jnp.bfloat16
    )
    d_up = (upstream * gate_float * logistic).astype(jnp.bfloat16)
    pieces = lax.all_gather(jnp.concatenate([d_gate, d_up], axis=1), "dp", axis=0, tiled=True)
    mine = lax.all_to_all(tokens, "dp", split_axis=1, concat_axis=0, tiled=True)
    columns = lax.all_gather(mine, "tp", axis=0, tiled=True)
    columns = columns.reshape(n_tp, n_dp, token_rows, width).transpose(1, 0, 2, 3)
    columns = columns.reshape(n_tp * n_dp * token_rows, width)
    across = (((1,), (1,)), ((), ()))
    contract = (((0,), (0,)), ((), ()))
    partial = (
        lax.dot_general(
            pieces[:, :hidden_width], gate_weight, across, preferred_element_type=jnp.float32
        )
        + lax.dot_general(
            pieces[:, hidden_width:], up_weight, across, preferred_element_type=jnp.float32
        )
    ).astype(jnp.bfloat16)
    partial = partial.reshape(n_dp, n_tp, token_rows, width).transpose(1, 0, 2, 3)
    partial = partial.reshape(n_tp * n_dp * token_rows, width)
    summed = lax.psum_scatter(partial, "tp", scatter_dimension=0, tiled=True)
    input_grad = lax.all_to_all(summed, "dp", split_axis=0, concat_axis=1, tiled=True)
    gate_grad = lax.dot_general(
        columns, pieces[:, :hidden_width], contract, preferred_element_type=jnp.float32
    ).astype(jnp.bfloat16)
    up_grad = lax.dot_general(
        columns, pieces[:, hidden_width:], contract, preferred_element_type=jnp.float32
    ).astype(jnp.bfloat16)
    return (input_grad, gate_grad, up_grad)


def solution(mesh):
    placed = (
        P(("dp", "tp"), None),
        P("dp", "tp"),
        P("dp", "tp"),
        P("dp", "tp"),
        P("dp", "tp"),
        P("dp", "tp"),
    )
    return jax.shard_map(
        on_device,
        mesh=mesh,
        in_specs=placed,
        out_specs=(P(("dp", "tp"), None), P("dp", "tp"), P("dp", "tp")),
        check_vma=False,
    )
```

profile of v0, /device:TPU:0, one launch (start us, length us, event | category | flops | bytes accessed | tf_op | source)
XLA Modules:
  0.0 198.5 jit_solution(8815059297840828324)
XLA Ops:
  7.2 0.0 all-gather.3.cloned.1.call-start
  7.2 2.2 %fusion.12 = (bf16[192,1792]{1,0:T(8,128)(2,1)S(1)}, bf16[192,1792]{1,0:T(8,128)(2,1)S(1)}) fusion(bf16[192,1792]{1,0:T(8,128)(2,1)} %param.7, bf16[192,1792]{1,0:T(8,128)(2,1)} %param.8, bf16[192,1792]{1,0:T(8,128)(2,1)} %param.9), kind=kLoop, calls=%fused_computation.17 | loop fusion | flops 5505024 | bytes 3440640 | tf_op jit(solution)/shard_map/convert_element_type | solution.py:17
  9.4 0.0 copy-start
  9.5 1.2 pad_maximum_fusion
  10.6 0.0 all-gather.3.cloned.1.call-update
  10.6 0.0 all-gather.5.cloned.1.call-start
  10.7 0.0 copy-done
  10.7 9.4 %all_to_all.38 = bf16[24,4,1024]{2,0,1:T(8,128)(2,1)} all-to-all(bf16[24,4,1024]{2,0,1:T(8,128)(2,1)S(1)} %bitcast.34), channel_id=1, replica_groups=mesh['tp'=8,'dp'=4] {'dp'}, dimensions={1} | all-to-all | bytes 393216 | tf_op jit(solution)/shard_map/all_to_all | solution.py:22
  20.2 0.0 all-gather.5.cloned.1.call-update
  20.2 0.0 reduce-scatter.2.cloned.1.call-start
  20.2 35.2 %all-gather.3.cloned.1.call-done = bf16[768,3584]{1,0:T(8,128)(2,1)} async-done(((bf16[192,3584]{1,0:T(8,128)(2,1)}), bf16[768,3584]{1,0:T(8,128)(2,1)}) %all-gather.3.cloned.1.call-update) | async-done | bytes 5505040 | tf_op jit(solution)/shard_map/all_gather | solution.py:21
  55.4 0.0 copy-start.1
  55.4 0.0 copy-start.2
  55.4 6.0 %fusion.3 = f32[768,1024]{1,0:T(8,128)S(1)} fusion(bf16[1024,1792]{1,0:T(8,128)(2,1)} %param.11, bf16[768,3584]{1,0:T(8,128)(2,1)} %all-gather.3.cloned.1.call-done), kind=kOutput, calls=%fused_computation.6 | convolution fusion | flops 2818572288 | bytes 9568256 | tf_op jit(solution)/shard_map/dot_general | solution.py:32
  61.5 0.0 copy-done.1
  61.5 0.0 copy-done.2
  61.5 3.0 %add_convert_fusion = bf16[768,1024]{1,0:T(8,128)(2,1)S(1)} fusion(f32[768,1024]{1,0:T(8,128)S(1)} %fusion.3, bf16[1024,1792]{1,0:T(8,128)(2,1)S(1)} %copy-done.2, bf16[768,3584]{1,0:T(8,128)(2,1)S(1)} %copy-done.1), kind=kOutput, calls=%fused_computation.4 | convolution fusion | flops 2820145152 | bytes 11141120 | tf_op jit(solution)/shard_map/dot_general | solution.py:29
  64.5 1.3 copy.21
  65.8 0.0 reduce-scatter.2.cloned.1.call-update
  65.8 36.0 %all-gather.5.cloned.1.call-done = bf16[768,1024]{1,0:T(8,128)(2,1)} async-done(((bf16[96,1024]{1,0:T(8,128)(2,1)}), bf16[768,1024]{1,0:T(8,128)(2,1)}) %all-gather.5.cloned.1.call-update) | async-done | bytes 1572880 | tf_op jit(solution)/shard_map/all_gather | solution.py:23
  101.8 1.6 copy.24
  103.4 6.4 %fusion = bf16[1024,1792]{0,1:T(8,128)(2,1)} fusion(bf16[768,1024]{1,0:T(8,128)(2,1)S(1)} %bitcast.29, bf16[768,3584]{1,0:T(8,128)(2,1)} %all-gather.3.cloned.1.call-done), kind=kOutput, calls=%fused_computation.2 | convolution fusion | flops 2820407296 | bytes 7995392 | tf_op jit(solution)/shard_map/dot_general | solution.py:40
  109.8 60.0 %reduce-scatter.2.cloned.1.call-done = bf16[96,1024]{1,0:T(8,128)(2,1)} async-done(((bf16[768,1024]{1,0:T(8,128)(2,1)}), bf16[96,1024]{1,0:T(8,128)(2,1)}) %reduce-scatter.2.cloned.1.call-update) | async-done | bytes 196624 | tf_op jit(solution)/shard_map/reduce_scatter | solution.py:38
  169.8 3.4 %all-to-all-start = ((bf16[4,24,1024]{2,1,0:T(8,128)(2,1)}), bf16[4,24,1024]{2,1,0:T(8,128)(2,1)S(1)}, u32[]{:S(2)}, u32[]{:S(2)}) async-start(bf16[4,24,1024]{2,1,0:T(8,128)(2,1)} %bitcast.36), calls=%async_computation.1 | async-start | bytes 393216 | tf_op jit(solution)/shard_map/all_to_all | solution.py:39
  173.1 6.3 %fusion.1 = bf16[1024,1792]{0,1:T(8,128)(2,1)} fusion(bf16[768,1024]{1,0:T(8,128)(2,1)S(1)} %bitcast.30, bf16[768,3584]{1,0:T(8,128)(2,1)} %all-gather.3.cloned.1.call-done), kind=kOutput, calls=%fused_computation.3 | convolution fusion | flops 2820407296 | bytes 7995392 | tf_op jit(solution)/shard_map/dot_general | solution.py:43
  179.4 5.9 %copy.26 = bf16[1024,1792]{1,0:T(8,128)(2,1)} copy(bf16[1024,1792]{0,1:T(8,128)(2,1)} %fusion.1) | data formatting | bytes 7340032
  185.3 5.9 %copy.25 = bf16[1024,1792]{1,0:T(8,128)(2,1)} copy(bf16[1024,1792]{0,1:T(8,128)(2,1)} %fusion) | data formatting | bytes 7340032
  191.3 0.0 all-to-all-done
  191.3 0.7 copy.28
  (1 shorter events, 0.0 us)
Async XLA Ops:
  7.2 48.3 %all-gather.3.cloned.1.call-start = ((), (), s32[]{:S(2)}) async-start(), calls=%async_computation.3 | async-start | bytes 6881280 | tf_op jit(solution)/shard_map/all_gather | solution.py:21
  9.4 1.3 copy-start
  10.6 91.2 %all-gather.5.cloned.1.call-start = ((), (), s32[]{:S(2)}) async-start(), calls=%async_computation.5 | async-start | bytes 1769472 | tf_op jit(solution)/shard_map/all_gather | solution.py:23
  20.2 149.6 %reduce-scatter.2.cloned.1.call-start = ((), (), s32[]{:S(2)}) async-start(), calls=%async_computation.4 | async-start | bytes 1769472 | tf_op jit(solution)/shard_map/reduce_scatter | solution.py:38
  55.4 6.1 %copy-start.1 = (bf16[768,3584]{1,0:T(8,128)(2,1)S(1)}, bf16[768,3584]{1,0:T(8,128)(2,1)}, u32[]{:S(2)}) copy-start(bf16[768,3584]{1,0:T(8,128)(2,1)} %all-gather.3.cloned.1.call-done) | copy-start | bytes 16515076
  55.4 6.1 %copy-start.2 = (bf16[1024,1792]{1,0:T(8,128)(2,1)S(1)}, bf16[1024,1792]{1,0:T(8,128)(2,1)}, u32[]{:S(2)}) copy-start(bf16[1024,1792]{1,0:T(8,128)(2,1)} %param.10) | copy-start | bytes 11010052
  169.8 21.5 %all-to-all-start = ((bf16[4,24,1024]{2,1,0:T(8,128)(2,1)}), bf16[4,24,1024]{2,1,0:T(8,128)(2,1)S(1)}, u32[]{:S(2)}, u32[]{:S(2)}) async-start(bf16[4,24,1024]{2,1,0:T(8,128)(2,1)} %bitcast.36), calls=%async_computation.1 | async-start | bytes 393216 | tf_op jit(solution)/shard_map/all_to_all | solution.py:39
Sparse Core Ops, SparseCore 0:
  10.8 44.6 all-gather.2
  57.6 44.1 all-gather.4
  105.8 63.8 reduce-scatter.1
where the time goes:
time: 199 us; the launch traced here: 198 us
  waiting for transfers between devices  131 us (66%)
  matrix products  21.8 us (11%)
  local copies, waits for them, and re-layouts  15.4 us (8%)
  between operations  13.8 us (7%)
  blocking collectives  9.44 us (5%)
  starting transfers between devices  3.49 us (2%)
  other arithmetic  3.4 us (2%)
    reduce_scatter x1, waiting for transfers between devices, on_device(): summed = lax.psum_scatter(partial, 'tp', scatter_dimension=0, tiled=True)  60 us
    all_gather x1, waiting for transfers between devices, on_device(): columns = lax.all_gather(mine, 'tp', axis=0, tiled=True)  36 us
    all_gather x1, waiting for transfers between devices, on_device(): lax.all_gather(jnp.concatenate([d_gate, d_up], axis=1), 'dp', axis=0, til...  35.2 us
    unnamed x8, local copies, waits for them, and re-layouts  11.8 us
    all_to_all x1, blocking collectives, on_device(): mine = lax.all_to_all(tokens, 'dp', split_axis=1, concat_axis=0, tiled=True)  9.44 us
    dot_general x1, matrix products, on_device(): lax.dot_general(columns, pieces[:, :hidden_width], contract, preferred_el...  6.42 us
    dot_general x1, matrix products, on_device(): lax.dot_general(columns, pieces[:, hidden_width:], contract, preferred_el...  6.3 us
    dot_general x1, matrix products, on_device(): lax.dot_general(pieces[:, hidden_width:], up_weight, across, preferred_el...  6.04 us
  transfers between devices with their start and end apart: 4, of which 3 were waited for; matrix products, arithmetic and copies ran while one was open for 18% of the time, Pallas kernels for 0%

commit v1 on v0

--- a/solution.py
+++ b/solution.py
@@ -20,7 +20,12 @@
     d_up = (upstream * gate_float * logistic).astype(jnp.bfloat16)
     pieces = lax.all_gather(jnp.concatenate([d_gate, d_up], axis=1), "dp", axis=0, tiled=True)
     mine = lax.all_to_all(tokens, "dp", split_axis=1, concat_axis=0, tiled=True)
-    columns = lax.all_gather(mine, "tp", axis=0, tiled=True)
+    ring = [mine]
+    for hop in range(7):
+        ring.append(lax.ppermute(ring[-1], "tp", [(dev, (dev + 1) % 8) for dev in range(8)]))
+    columns = jnp.roll(
+        jnp.concatenate(ring[::-1], axis=0), (lax.axis_index("tp") + 1) * ring[0].shape[0], axis=0
+    )
     columns = columns.reshape(n_tp, n_dp, token_rows, width).transpose(1, 0, 2, 3)
     columns = columns.reshape(n_tp * n_dp * token_rows, width)
     across = (((1,), (1,)), ((), ()))

time: 199 us -> 151 us (0.76)
  waiting for transfers between devices: 131 us -> 92.3 us
  local copies, waits for them, and re-layouts: 15.4 us -> 2.8 us
  starting transfers between devices: 3.49 us -> 6.51 us
    ppermute x0 -> x7, waiting for transfers between devices: none -> 54.8 us  [on_device(): lax.ppermute(ring[-1], 'tp', [(dev, (dev + 1) % 8) for dev in range(8)])]
    all_gather x1 -> x0, waiting for transfers between devices: 36 us -> none  [on_device(): columns = lax.all_gather(mine, 'tp', axis=0, tiled=True)]
    all_gather x1, waiting for transfers between devices: 35.2 us -> 0.7 us  [on_device(): lax.all_gather(jnp.concatenate([d_gate, d_up], axis=1), 'dp', axis=0, til...]
    reduce_scatter x1, waiting for transfers between devices: 60 us -> 36.7 us  [on_device(): summed = lax.psum_scatter(partial, 'tp', scatter_dimension=0, tiled=True)]
    unnamed x8 -> x21, local copies, waits for them, and re-layouts: 11.8 us -> 0.24 us
    ppermute x0 -> x7, starting transfers between devices: none -> 3.06 us  [on_device(): lax.ppermute(ring[-1], 'tp', [(dev, (dev + 1) % 8) for dev in range(8)])]
  transfers between devices with their start and end apart: 4 -> 10, of which waited for: 3 -> 8; matrix products, arithmetic and copies ran while one was open for 18% -> 16% of each run, Pallas kernels for 0% -> 0%
where the time goes in v1:
time: 151 us; the launch traced here: 150 us
  waiting for transfers between devices  92.3 us (61%)
  matrix products  21.7 us (14%)
  between operations  14.3 us (9%)
  blocking collectives  9.34 us (6%)
  starting transfers between devices  6.51 us (4%)
  other arithmetic  3.43 us (2%)
  local copies, waits for them, and re-layouts  2.8 us (2%)
    ppermute x7, waiting for transfers between devices, on_device(): lax.ppermute(ring[-1], 'tp', [(dev, (dev + 1) % 8) for dev in range(8)])  54.8 us
    reduce_scatter x1, waiting for transfers between devices, on_device(): summed = lax.psum_scatter(partial, 'tp', scatter_dimension=0, tiled=True)  36.7 us
    all_to_all x1, blocking collectives, on_device(): mine = lax.all_to_all(tokens, 'dp', split_axis=1, concat_axis=0, tiled=True)  9.34 us
    dot_general x1, matrix products, on_device(): lax.dot_general(columns, pieces[:, hidden_width:], contract, preferred_el...  6.33 us
    dot_general x1, matrix products, on_device(): lax.dot_general(columns, pieces[:, :hidden_width], contract, preferred_el...  6.33 us
    dot_general x1, matrix products, on_device(): lax.dot_general(pieces[:, hidden_width:], up_weight, across, preferred_el...  6.04 us
    all_to_all x1, starting transfers between devices, on_device(): lax.all_to_all(summed, 'dp', split_axis=0, concat_axis=1, tiled=True)  3.36 us
    ppermute x7, starting transfers between devices, on_device(): lax.ppermute(ring[-1], 'tp', [(dev, (dev + 1) % 8) for dev in range(8)])  3.06 us
  transfers between devices with their start and end apart: 10, of which 8 were waited for; matrix products, arithmetic and copies ran while one was open for 16% of the time, Pallas kernels for 0%

profile of v1, /device:TPU:0, one launch (start us, length us, event | category | flops | bytes accessed | tf_op | source)
XLA Modules:
  0.0 150.3 jit_solution(9949181267962892560)
XLA Ops:
  7.2 0.0 all-gather.2.cloned.1.call-start
  7.2 2.3 %fusion.10 = (bf16[192,1792]{1,0:T(8,128)(2,1)S(1)}, bf16[192,1792]{1,0:T(8,128)(2,1)S(1)}) fusion(bf16[192,1792]{1,0:T(8,128)(2,1)} %param.7, bf16[192,1792]{1,0:T(8,128)(2,1)} %param.8, bf16[192,1792]{1,0:T(8,128)(2,1)} %param.9), kind=kLoop, calls=%fused_computation.15 | loop fusion | flops 5505024 | bytes 3440640 | tf_op jit(solution)/shard_map/convert_element_type | solution.py:17
  9.5 1.2 pad_maximum_fusion
  10.7 0.0 all-gather.2.cloned.1.call-update
  10.7 0.0 reduce-scatter.2.cloned.1.call-start
  10.8 9.3 %all_to_all.38 = bf16[24,4,1024]{2,0,1:T(8,128)(2,1)S(1)} all-to-all(bf16[24,4,1024]{2,0,1:T(8,128)(2,1)S(1)} %bitcast.32), channel_id=1, replica_groups=mesh['tp'=8,'dp'=4] {'dp'}, dimensions={1} | all-to-all | bytes 393216 | tf_op jit(solution)/shard_map/all_to_all | solution.py:22
  20.1 1.5 %collective-permute-start = (bf16[96,1024]{1,0:T(8,128)(2,1)S(1)}, bf16[96,1024]{1,0:T(8,128)(2,1)S(1)}, u32[]{:S(2)}, u32[]{:S(2)}) collective-permute-start(bf16[96,1024]{1,0:T(8,128)(2,1)S(1)} %bitcast.25), channel_id=1, source_target_pairs={{0,4},{4,8},{8,12},{12,16},{16,20},{20,24},{24,28},{28,0},{1,5},{5... | collective-permute-start | bytes 589832 | tf_op jit(solution)/shard_map/ppermute | solution.py:25
  21.6 7.9 %collective-permute-done = bf16[96,1024]{1,0:T(8,128)(2,1)S(1)} collective-permute-done((bf16[96,1024]{1,0:T(8,128)(2,1)S(1)}, bf16[96,1024]{1,0:T(8,128)(2,1)S(1)}, u32[]{:S(2)}, u32[]{:S(2)}) %collective-permute-start) | collective-permute-done | bytes 196640 | tf_op jit(solution)/shard_map/ppermute | solution.py:25
  29.5 0.0 collective-permute-start.1
  29.5 8.5 %collective-permute-done.1 = bf16[96,1024]{1,0:T(8,128)(2,1)S(1)} collective-permute-done((bf16[96,1024]{1,0:T(8,128)(2,1)S(1)}, bf16[96,1024]{1,0:T(8,128)(2,1)S(1)}, u32[]{:S(2)}, u32[]{:S(2)}) %collective-permute-start.1) | collective-permute-done | bytes 196640 | tf_op jit(solution)/shard_map/ppermute | solution.py:25
  38.0 0.0 collective-permute-start.2
  38.0 8.4 %collective-permute-done.2 = bf16[96,1024]{1,0:T(8,128)(2,1)S(1)} collective-permute-done((bf16[96,1024]{1,0:T(8,128)(2,1)S(1)}, bf16[96,1024]{1,0:T(8,128)(2,1)S(1)}, u32[]{:S(2)}, u32[]{:S(2)}) %collective-permute-start.2) | collective-permute-done | bytes 196640 | tf_op jit(solution)/shard_map/ppermute | solution.py:25
  46.4 0.0 collective-permute-start.3
  46.4 8.4 %collective-permute-done.3 = bf16[96,1024]{1,0:T(8,128)(2,1)S(1)} collective-permute-done((bf16[96,1024]{1,0:T(8,128)(2,1)S(1)}, bf16[96,1024]{1,0:T(8,128)(2,1)S(1)}, u32[]{:S(2)}, u32[]{:S(2)}) %collective-permute-start.3) | collective-permute-done | bytes 196640 | tf_op jit(solution)/shard_map/ppermute | solution.py:25
  54.7 0.0 collective-permute-start.4
  54.8 0.7 all-gather.2.cloned.1.call-done
  55.5 6.0 %fusion.1 = f32[768,1024]{1,0:T(8,128)S(1)} fusion(bf16[1024,1792]{1,0:T(8,128)(2,1)} %param.11, bf16[768,3584]{1,0:T(8,128)(2,1)} %all-gather.2.cloned.1.call-done), kind=kOutput, calls=%fused_computation.4 | convolution fusion | flops 2818572288 | bytes 9568256 | tf_op jit(solution)/shard_map/dot_general | solution.py:37
  61.5 3.0 %add_convert_fusion = bf16[768,1024]{1,0:T(8,128)(2,1)S(1)} fusion(f32[768,1024]{1,0:T(8,128)S(1)} %fusion.1, bf16[1024,1792]{1,0:T(8,128)(2,1)S(1)} %copy-done.2, bf16[768,3584]{1,0:T(8,128)(2,1)S(1)} %copy-done.1), kind=kOutput, calls=%fused_computation.2 | convolution fusion | flops 2820145152 | bytes 11141120 | tf_op jit(solution)/shard_map/dot_general | solution.py:34
  64.6 1.3 copy.14
  65.8 0.0 reduce-scatter.2.cloned.1.call-update
  65.8 0.0 collective-permute-done.4
  65.9 1.5 %collective-permute-start.5 = (bf16[96,1024]{1,0:T(8,128)(2,1)S(1)}, bf16[96,1024]{1,0:T(8,128)(2,1)S(1)}, u32[]{:S(2)}, u32[]{:S(2)}) collective-permute-start(bf16[96,1024]{1,0:T(8,128)(2,1)S(1)} %collective-permute-done.4), channel_id=1, source_target_pairs={{0,4},{4,8},{8,12},{12,16},{16,20},{20,24},{24,28},{28,0},{1,5},{5... | collective-permute-start | bytes 589832 | tf_op jit(solution)/shard_map/ppermute | solution.py:25
  67.4 8.3 %collective-permute-done.5 = bf16[96,1024]{1,0:T(8,128)(2,1)S(1)} collective-permute-done((bf16[96,1024]{1,0:T(8,128)(2,1)S(1)}, bf16[96,1024]{1,0:T(8,128)(2,1)S(1)}, u32[]{:S(2)}, u32[]{:S(2)}) %collective-permute-start.5) | collective-permute-done | bytes 196640 | tf_op jit(solution)/shard_map/ppermute | solution.py:25
  75.7 13.4 %collective-permute-done.6 = bf16[96,1024]{1,0:T(8,128)(2,1)S(1)} collective-permute-done((bf16[96,1024]{1,0:T(8,128)(2,1)S(1)}, bf16[96,1024]{1,0:T(8,128)(2,1)S(1)}, u32[]{:S(2)}, u32[]{:S(2)}) %collective-permute-start.6) | collective-permute-done | bytes 196640 | tf_op jit(solution)/shard_map/ppermute | solution.py:25
  89.5 0.4 constant_dynamic-slice_fusion
  89.9 0.1 copy.17
  90.0 6.3 %convolution_convert_fusion = bf16[1024,1792]{1,0:T(8,128)(2,1)} fusion(bf16[768,1024]{1,0:T(8,128)(2,1)S(1)} %bitcast.28, bf16[768,3584]{1,0:T(8,128)(2,1)} %all-gather.2.cloned.1.call-done), kind=kOutput, calls=%fused_computation | convolution fusion | flops 2820407296 | bytes 7995392 | tf_op jit(solution)/shard_map/dot_general | solution.py:48
  96.4 36.7 %reduce-scatter.2.cloned.1.call-done = bf16[96,1024]{1,0:T(8,128)(2,1)} async-done(((bf16[768,1024]{1,0:T(8,128)(2,1)}), bf16[96,1024]{1,0:T(8,128)(2,1)}) %reduce-scatter.2.cloned.1.call-update) | async-done | bytes 196624 | tf_op jit(solution)/shard_map/reduce_scatter | solution.py:43
  133.1 3.4 %all-to-all-start = ((bf16[4,24,1024]{2,1,0:T(8,128)(2,1)}), bf16[4,24,1024]{2,1,0:T(8,128)(2,1)S(1)}, u32[]{:S(2)}, u32[]{:S(2)}) async-start(bf16[4,24,1024]{2,1,0:T(8,128)(2,1)} %bitcast.34), calls=%async_computation.1 | async-start | bytes 393216 | tf_op jit(solution)/shard_map/all_to_all | solution.py:44
  136.5 6.3 %convolution_convert_fusion.1 = bf16[1024,1792]{1,0:T(8,128)(2,1)} fusion(bf16[768,1024]{1,0:T(8,128)(2,1)S(1)} %bitcast.29, bf16[768,3584]{1,0:T(8,128)(2,1)} %all-gather.2.cloned.1.call-done), kind=kOutput, calls=%fused_computation.1 | convolution fusion | flops 2820407296 | bytes 7995392 | tf_op jit(solution)/shard_map/dot_general | solution.py:45
  142.8 0.0 all-to-all-done
  142.8 0.7 copy.19
  (24 shorter events, 0.3 us)
Async XLA Ops:
  7.2 3.6 %copy-start = (bf16[24,4096]{1,0:T(8,128)(2,1)S(1)}, bf16[24,4096]{1,0:T(8,128)(2,1)}, u32[]{:S(2)}) copy-start(bf16[24,4096]{1,0:T(8,128)(2,1)} %param.6) | copy-start | bytes 589828
  7.2 48.3 %all-gather.2.cloned.1.call-start = ((), (), s32[]{:S(2)}) async-start(), calls=%async_computation.3 | async-start | bytes 6881280 | tf_op jit(solution)/shard_map/all_gather | solution.py:21
  10.7 122.4 %reduce-scatter.2.cloned.1.call-start = ((), (), s32[]{:S(2)}) async-start(), calls=%async_computation.4 | async-start | bytes 1769472 | tf_op jit(solution)/shard_map/reduce_scatter | solution.py:43
  20.1 9.4 %collective-permute-start = (bf16[96,1024]{1,0:T(8,128)(2,1)S(1)}, bf16[96,1024]{1,0:T(8,128)(2,1)S(1)}, u32[]{:S(2)}, u32[]{:S(2)}) collective-permute-start(bf16[96,1024]{1,0:T(8,128)(2,1)S(1)} %bitcast.25), channel_id=1, source_target_pairs={{0,4},{4,8},{8,12},{12,16},{16,20},{20,24},{24,28},{28,0},{1,5},{5... | collective-permute-start | bytes 589832 | tf_op jit(solution)/shard_map/ppermute | solution.py:25
  29.5 8.5 %collective-permute-start.1 = (bf16[96,1024]{1,0:T(8,128)(2,1)S(1)}, bf16[96,1024]{1,0:T(8,128)(2,1)S(1)}, u32[]{:S(2)}, u32[]{:S(2)}) collective-permute-start(bf16[96,1024]{1,0:T(8,128)(2,1)S(1)} %collective-permute-done), channel_id=1, source_target_pairs={{0,4},{4,8},{8,12},{12,16},{16,20},{20,24},{24,28},{28,0},{1,5},{5... | collective-permute-start | bytes 589832 | tf_op jit(solution)/shard_map/ppermute | solution.py:25
  38.0 8.4 %collective-permute-start.2 = (bf16[96,1024]{1,0:T(8,128)(2,1)S(1)}, bf16[96,1024]{1,0:T(8,128)(2,1)S(1)}, u32[]{:S(2)}, u32[]{:S(2)}) collective-permute-start(bf16[96,1024]{1,0:T(8,128)(2,1)S(1)} %collective-permute-done.1), channel_id=1, source_target_pairs={{0,4},{4,8},{8,12},{12,16},{16,20},{20,24},{24,28},{28,0},{1,5},{5... | collective-permute-start | bytes 589832 | tf_op jit(solution)/shard_map/ppermute | solution.py:25
  46.4 8.4 %collective-permute-start.3 = (bf16[96,1024]{1,0:T(8,128)(2,1)S(1)}, bf16[96,1024]{1,0:T(8,128)(2,1)S(1)}, u32[]{:S(2)}, u32[]{:S(2)}) collective-permute-start(bf16[96,1024]{1,0:T(8,128)(2,1)S(1)} %collective-permute-done.2), channel_id=1, source_target_pairs={{0,4},{4,8},{8,12},{12,16},{16,20},{20,24},{24,28},{28,0},{1,5},{5... | collective-permute-start | bytes 589832 | tf_op jit(solution)/shard_map/ppermute | solution.py:25
  54.7 11.1 %collective-permute-start.4 = (bf16[96,1024]{1,0:T(8,128)(2,1)S(1)}, bf16[96,1024]{1,0:T(8,128)(2,1)S(1)}, u32[]{:S(2)}, u32[]{:S(2)}) collective-permute-start(bf16[96,1024]{1,0:T(8,128)(2,1)S(1)} %collective-permute-done.3), channel_id=1, source_target_pairs={{0,4},{4,8},{8,12},{12,16},{16,20},{20,24},{24,28},{28,0},{1,5},{5... | collective-permute-start | bytes 589832 | tf_op jit(solution)/shard_map/ppermute | solution.py:25
  55.5 6.1 %copy-start.1 = (bf16[768,3584]{1,0:T(8,128)(2,1)S(1)}, bf16[768,3584]{1,0:T(8,128)(2,1)}, u32[]{:S(2)}) copy-start(bf16[768,3584]{1,0:T(8,128)(2,1)} %all-gather.2.cloned.1.call-done) | copy-start | bytes 16515076
  55.5 6.1 %copy-start.2 = (bf16[1024,1792]{1,0:T(8,128)(2,1)S(1)}, bf16[1024,1792]{1,0:T(8,128)(2,1)}, u32[]{:S(2)}) copy-start(bf16[1024,1792]{1,0:T(8,128)(2,1)} %param.10) | copy-start | bytes 11010052
  65.9 9.9 %collective-permute-start.5 = (bf16[96,1024]{1,0:T(8,128)(2,1)S(1)}, bf16[96,1024]{1,0:T(8,128)(2,1)S(1)}, u32[]{:S(2)}, u32[]{:S(2)}) collective-permute-start(bf16[96,1024]{1,0:T(8,128)(2,1)S(1)} %collective-permute-done.4), channel_id=1, source_target_pairs={{0,4},{4,8},{8,12},{12,16},{16,20},{20,24},{24,28},{28,0},{1,5},{5... | collective-permute-start | bytes 589832 | tf_op jit(solution)/shard_map/ppermute | solution.py:25
  75.7 13.4 %collective-permute-start.6 = (bf16[96,1024]{1,0:T(8,128)(2,1)S(1)}, bf16[96,1024]{1,0:T(8,128)(2,1)S(1)}, u32[]{:S(2)}, u32[]{:S(2)}) collective-permute-start(bf16[96,1024]{1,0:T(8,128)(2,1)S(1)} %collective-permute-done.5), channel_id=1, source_target_pairs={{0,4},{4,8},{8,12},{12,16},{16,20},{20,24},{24,28},{28,0},{1,5},{5... | collective-permute-start | bytes 589832 | tf_op jit(solution)/shard_map/ppermute | solution.py:25
  133.1 9.7 %all-to-all-start = ((bf16[4,24,1024]{2,1,0:T(8,128)(2,1)}), bf16[4,24,1024]{2,1,0:T(8,128)(2,1)S(1)}, u32[]{:S(2)}, u32[]{:S(2)}) async-start(bf16[4,24,1024]{2,1,0:T(8,128)(2,1)} %bitcast.34), calls=%async_computation.1 | async-start | bytes 393216 | tf_op jit(solution)/shard_map/all_to_all | solution.py:44
Sparse Core Ops, SparseCore 0:
  10.8 44.6 all-gather.1
  66.0 67.0 reduce-scatter.1
